TPU v7x, 32 devices: a whole 2x2x4 slice. The times are simulated.
32 devices in a mesh: row: 4 (over z), col: 8 (over y, x, core).
Axes of the slice: x: 2, y: 2, z: 4, core: 2. Of those that a mesh axis runs over, the one named last changes fastest.
Arguments:
- right_side: float32 [3, 24576], P(None, ('row', 'col'))
- linewidth: float32 [24576], P(('row', 'col')), may hold values from 0.6 to 2.4
- scattering: float32 [24576, 24576], P('row', 'col'), as said below
Outputs:
- solution: float32 [3, 24576], P(None, ('row', 'col'))
- residual: float32 [3, 24576], P(None, ('row', 'col'))
Inputs may be any that keep to these rules, and one draw needn't show every extreme that they name: scattering is symmetric.
All inputs are finite; a program needn't handle non-finite values.
Results may differ from a plain program's by a relative error of at most 0.00018.
Values sent between devices are 32-bit elements; how exact they have to be, the bound alone decides.
No kernel may reach another device: no remote copies, remote signals or barrier semaphores. Data moves between devices by JAX's collectives and lax.ppermute only.
A program may use at most 128 MiB of HBM per device.

v0:
```python
import jax
import jax.numpy as jnp
from jax import lax
from jax.sharding import PartitionSpec as P

ITERS = 2


def apply_operator(vectors, linewidth, scattering):
    block_cols = scattering.shape[1]
    column_index = lax.axis_index("col")
    gathered = lax.all_gather(vectors, ("row", "col"), axis=1, tiled=True)
    columns = lax.dynamic_slice_in_dim(gathered, column_index * block_cols, block_cols, 1)
    partial_terms = lax.dot_general(
        columns,
        scattering,
        (((1,), (1,)), ((), ())),
        precision=lax.Precision.HIGHEST,
        preferred_element_type=jnp.float32,
    )
    summed = lax.psum_scatter(partial_terms, "col", scatter_dimension=1, tiled=True)
    return linewidth[None, :] * vectors + summed


def two_products(residual, image):
    return lax.psum(
        (jnp.sum(residual * residual, axis=1), jnp.sum(residual * image, axis=1)), ("row", "col")
    )


def body(right_side, linewidth, scattering):
    solution = jnp.zeros_like(right_side)
    residual = right_side
    image = apply_operator(residual, linewidth, scattering)
    norm_now, product = two_products(residual, image)
    step_size = norm_now / product
    direction = residual
    along = image
    for iteration in range(ITERS):
        solution = solution + step_size[:, None] * direction
        residual = residual - step_size[:, None] * along
        if iteration + 1 < ITERS:
            image = apply_operator(residual, linewidth, scattering)
            norm_next, product = two_products(residual, image)
            factor = norm_next / norm_now
            step_size = norm_next / (product - factor * norm_next / step_size)
            direction = residual + factor[:, None] * direction
            along = image + factor[:, None] * along
            norm_now = norm_next
    return (solution, residual)


def solution(mesh):
    placed = (P(None, ("row", "col")), P(("row", "col")), P("row", "col"))
    return jax.shard_map(
        body,
        mesh=mesh,
        in_specs=placed,
        out_specs=(P(None, ("row", "col")), P(None, ("row", "col"))),
        check_vma=False,
    )
```

profile of v0, /device:TPU:0, one launch (start us, length us, event | category | flops | bytes accessed | tf_op | source)
XLA Modules:
  0.0 395.6 jit_solution(1301404878924223556)
XLA Ops:
  7.2 0.0 copy-start
  7.2 0.0 copy-start.1
  7.2 0.0 reduce-scatter.7.cloned.1.call-start
  7.2 44.6 %all_gather.6 = f32[3,24576]{1,0:T(4,128)S(1)} all-gather(f32[3,768]{1,0:T(4,128)} %param.3), channel_id=1, replica_groups=mesh['row'=4,'col'=8] {'row','col'}, dimensions={1}, use_global_device_ids=true | all-gather | bytes 304128 | tf_op jit(solution)/shard_map/all_gather | solution.py:12
  51.8 63.9 %convolution_bitcast_fusion.1 = f32[6144,3]{1,0:T(8,128)} fusion(f32[6144,3072]{1,0:T(8,128)} %param.5, f32[3,24576]{1,0:T(4,128)S(1)} %all_gather.6, s32[]{:T(128)S(6)} %select_n.4), kind=kOutput, calls=%fused_computation.1 | convolution fusion | flops 679477248 | bytes 75620352
  115.7 0.0 reduce-scatter.7.cloned.1.call-update
  115.7 0.0 reduce-scatter.9.cloned.1.call-start
  115.8 42.3 %reduce-scatter.7.cloned.1.call-done = f32[768,3]{1,0:T(8,128)} async-done(((f32[6144,3]{1,0:T(8,128)}), f32[768,3]{1,0:T(8,128)}) %reduce-scatter.7.cloned.1.call-update) | async-done | bytes 9232
  158.1 1.1 copy.6
  159.2 0.0 copy-done
  159.2 0.0 copy-done.1
  159.2 0.2 multiply_reduce_fusion.2
  159.4 39.3 %all-reduce.1 = (f32[3]{0:T(128)S(1)}, f32[3]{0:T(128)S(1)}) all-reduce(f32[3]{0:T(128)S(1)} %get-tuple-element.5, f32[3]{0:T(128)S(1)} %get-tuple-element.4), channel_id=1, replica_groups=mesh['row'=4,'col'=8] {'row','col'}, use_global_device_ids=true, to_apply=%region_1.0 | all-reduce | flops 6 | bytes 48 | tf_op jit(solution)/shard_map/psum | solution.py:26
  198.7 0.1 multiply_subtract_fusion.1
  198.7 42.4 %all_gather.7 = f32[3,24576]{1,0:T(4,128)S(1)} all-gather(f32[3,768]{1,0:T(4,128)S(1)} %multiply_subtract_fusion.1), channel_id=1, replica_groups=mesh['row'=4,'col'=8] {'row','col'}, dimensions={1}, use_global_device_ids=true | all-gather | bytes 304128 | tf_op jit(solution)/shard_map/all_gather | solution.py:12
  241.1 63.9 %convolution_bitcast_fusion = f32[6144,3]{1,0:T(8,128)} fusion(f32[6144,3072]{1,0:T(8,128)} %param.5, f32[3,24576]{1,0:T(4,128)S(1)} %all_gather.7, s32[]{:T(128)S(6)} %select_n.4), kind=kOutput, calls=%fused_computation | convolution fusion | flops 679477248 | bytes 75620352
  305.0 0.0 reduce-scatter.9.cloned.1.call-update
  305.1 42.3 %reduce-scatter.9.cloned.1.call-done = f32[768,3]{1,0:T(8,128)} async-done(((f32[6144,3]{1,0:T(8,128)}), f32[768,3]{1,0:T(8,128)}) %reduce-scatter.9.cloned.1.call-update) | async-done | bytes 9232
  347.4 1.1 copy.8
  348.5 0.2 multiply_reduce_fusion
  348.7 39.3 %all-reduce = (f32[3]{0:T(128)S(1)}, f32[3]{0:T(128)S(1)}) all-reduce(f32[3]{0:T(128)S(1)} %get-tuple-element.3, f32[3]{0:T(128)S(1)} %get-tuple-element.2), channel_id=1, replica_groups=mesh['row'=4,'col'=8] {'row','col'}, use_global_device_ids=true, to_apply=%region_6.0 | all-reduce | flops 6 | bytes 48 | tf_op jit(solution)/shard_map/psum | solution.py:26
  388.0 0.7 multiply_subtract_fusion
  (2 shorter events, 0.0 us)
Async XLA Ops:
  7.2 152.0 %copy-start = (f32[3,768]{1,0:T(4,128)S(1)}, f32[3,768]{1,0:T(4,128)}, u32[]{:S(2)}) copy-start(f32[3,768]{1,0:T(4,128)} %param.3) | copy-start | bytes 27652
  7.2 152.0 %copy-start.1 = (f32[768]{0:T(1024)S(1)}, f32[768]{0:T(1024)}, u32[]{:S(2)}) copy-start(f32[768]{0:T(1024)} %param.4) | copy-start | bytes 9220
  7.2 150.9 %reduce-scatter.7.cloned.1.call-start = ((), (), s32[]{:S(2)}) async-start(), calls=%async_computation.2 | async-start | bytes 3538944
  115.7 231.7 %reduce-scatter.9.cloned.1.call-start = ((), (), s32[]{:S(2)}) async-start(), calls=%async_computation.3 | async-start | bytes 3538944
Sparse Core Ops, SparseCore 0:
  115.8 42.1 reduce-scatter.6
  305.2 42.1 reduce-scatter.8
where the time goes:
time: 396 us
  blocking collectives  166 us (42%)
  matrix products  128 us (32%)
  waiting for transfers between devices  84.7 us (21%)
  between operations  14.1 us (4%)
    unnamed x2, matrix products  128 us
    all_gather x2, blocking collectives, apply_operator(): gathered = lax.all_gather(vectors, ('row', 'col'), axis=1, tiled=True)  87 us
    unnamed x4, waiting for transfers between devices  84.7 us
    psum x2, blocking collectives, two_products(): lax.psum((jnp.sum(residual * residual, axis=1), jnp.sum(residual * image,...  78.6 us
  transfers between devices with their start and end apart: 2, of which 2 were waited for; matrix products, arithmetic and copies ran while one was open for 0% of the time, Pallas kernels for 0%

commit v1 on v0

v1 whole, which is shorter than its diff:
```python
import functools

import jax
import jax.numpy as jnp
from jax import lax
from jax.experimental import pallas as pl
from jax.experimental.pallas import tpu as pltpu
from jax.sharding import PartitionSpec as P

LANES = 128
SUB = 8
BL = 128
CH = 256
RHS = 3
FIRST = 3
SECOND = 6
THIRD = 5
SLOTS = 4
AHEAD = 4

HBM = pl.BlockSpec(memory_space=pltpu.HBM)
VMEM = pl.BlockSpec(memory_space=pltpu.VMEM)


def on_chip(x):
    return pltpu.with_memory_space_constraint(x, pltpu.VMEM)


def row_of(chunk, flip, per_block):
    block = lax.bitwise_xor(chunk // per_block, flip)
    return pl.multiple_of((block * per_block + lax.rem(chunk, per_block)) * CH, CH)


def call(kernel, name, out, limit, ins, scratch=(), **kw):
    return pl.pallas_call(
        kernel,
        name=name,
        in_specs=[HBM if space == "hbm" else VMEM for space in ins],
        out_specs=jax.tree.map(lambda _: VMEM, out),
        out_shape=out,
        scratch_shapes=list(scratch),
        compiler_params=pltpu.CompilerParams(vmem_limit_bytes=limit << 20),
        **kw,
    )


def prefetch_kernel(first, count, flip_of, per_block, s_hbm, after, keep, sem):
    flip = flip_of()
    copies = []
    for i in range(count):
        row = row_of(jnp.int32(first + i), flip, per_block)
        copies.append(
            pltpu.make_async_copy(
                s_hbm.at[pl.ds(row, CH)], keep.at[pl.ds(i * CH, CH)], sem.at[i]
            )
        )
        copies[-1].start()
    for c in copies:
        c.wait()


def merge_kernel(a, b, out):
    out[0:4, :] = a[...]
    out[4:8, :] = b[...]


def spread(v, vb, start):
    t = jnp.transpose(v[:, pl.ds(pl.multiple_of(start, BL), BL)])
    for k in range(RHS):
        vb[k] = jnp.broadcast_to(t[:, k : k + 1], (BL, LANES))


def rows_block(src, row, vb, acc, tiles, v, next_vb, next_start):
    half = tiles // 2
    for h in range(0, tiles, half):
        cols = [slice(c * LANES, (c + 1) * LANES) for c in range(h, h + half)]
        a = [[acc[k, :, c] for c in cols] for k in range(RHS)]
        for g in range(BL // SUB):
            b = [vb[k, g * SUB : (g + 1) * SUB, :] for k in range(RHS)]
            for j, c in enumerate(cols):
                t = src[pl.ds(row + g * SUB, SUB), c]
                for k in range(RHS):
                    a[k][j] = a[k][j] + t * b[k]
        for k in range(RHS):
            for j, c in enumerate(cols):
                acc[k, :, c] = a[k][j]
        if h == 0:
            spread(v, next_vb, next_start)


def cols_block(src, row, wb, part, tiles):
    rows = BL // 2
    for h in range(0, BL, rows):
        a = [jnp.zeros((rows, LANES), jnp.float32)] * RHS
        for c in range(tiles):
            t = src[pl.ds(row + h, rows), c * LANES : (c + 1) * LANES]
            for k in range(RHS):
                b = jnp.concatenate([wb[k * tiles + c]] * (rows // SUB), axis=0)
                a[k] = a[k] + t * b
        for k in range(RHS):
            part[k, h : h + rows, :] = a[k]


def cols_finish(part, zs, block, lane):
    for k in range(RHS):
        total = jnp.sum(jnp.transpose(part[k]), axis=0, keepdims=True)
        zs[block, k : k + 1, pl.ds(pl.multiple_of(lane, BL), BL)] = total


def stream(s_hbm, ring, sem, keep, keep_sem, first, kept, total, flip, per_block, visit):
    def kept_copy(i):
        return pltpu.make_async_copy(
            s_hbm.at[pl.ds(row_of(first + i, flip, per_block), CH)],
            keep.at[pl.ds(pl.multiple_of(i * CH, CH), CH)],
            keep_sem.at[i],
        )

    def ring_copy(i):
        slot = lax.rem(i, SLOTS)
        return pltpu.make_async_copy(
            s_hbm.at[pl.ds(row_of(first + kept + i, flip, per_block), CH)],
            ring.at[slot],
            sem.at[slot],
        )

    rest = total - first - kept

    def start():
        for i in range(min(AHEAD, kept)):
            kept_copy(jnp.int32(i)).start()
        for i in range(min(SLOTS, rest, SLOTS if kept == 0 else max(0, AHEAD - kept))):
            ring_copy(jnp.int32(i)).start()

    begun = min(SLOTS, rest, SLOTS if kept == 0 else max(0, AHEAD - kept))

    def run():
        def kept_step(i, _):
            kept_copy(i).wait()

            @pl.when(i + AHEAD < kept)
            def _():
                kept_copy(i + AHEAD).start()

            if rest > 0:
                ahead = i + AHEAD - kept

                @pl.when((ahead >= begun) & (ahead < min(SLOTS, rest)))
                def _():
                    ring_copy(ahead).start()

            visit(keep, i * CH, first + i)
            return 0

        if kept:
            lax.fori_loop(0, kept, kept_step, 0)

        def ring_step(i, _):
            ring_copy(i).wait()
            visit(ring.at[lax.rem(i, SLOTS)], 0, first + kept + i)

            @pl.when(i + SLOTS < rest)
            def _():
                ring_copy(i + SLOTS).start()

            return 0

        if rest:
            lax.fori_loop(0, rest, ring_step, 0)

    return start, run


def rows_kernel(geo, *refs):
    (nb, blocks, own_blocks, tiles, per_block, counts, total, flip_of, off_of) = geo
    n_keep = sum(1 for c in counts[:2] if c)
    s_hbm, *rest = refs
    keeps = rest[:n_keep]
    pieces = rest[n_keep : n_keep + blocks // 2]
    rest = rest[n_keep + blocks // 2 :]
    if counts[2]:
        out, keep, ring, acc, vb0, vb1, v, keep_sem, sem = rest
    else:
        out, ring, acc, vb0, vb1, v, sem = rest
        keep = keep_sem = None
    flip = flip_of()
    first = counts[0] + counts[1]

    def visit(src, row, chunk):
        at = chunk * CH
        rows_block(src, row, vb0, acc, tiles, v, vb1, at + BL)
        following = jnp.minimum(at + CH, (total - 1) * CH)
        rows_block(src, row + BL, vb1, acc, tiles, v, vb0, following)

    start, run = stream(
        s_hbm, ring, sem, keep, keep_sem, first, counts[2], total, flip, per_block, visit
    )
    start()
    v[4:8, :] = jnp.zeros_like(v[4:8, :])
    for i, piece in enumerate(pieces):
        v[0:4, 2 * i * nb : (2 * i + 1) * nb] = piece[0:4, :]
        v[0:4, (2 * i + 1) * nb : (2 * i + 2) * nb] = piece[4:8, :]
    acc[...] = jnp.zeros_like(acc)
    out[...] = jnp.zeros_like(out)
    spread(v, vb0, jnp.int32(0))
    at = 0
    for ref, count in zip(keeps, [c for c in counts[:2] if c]):

        def step(i, _, ref=ref, at=at):
            visit(ref, i * CH, at + i)
            return 0

        lax.fori_loop(0, count, step, 0)
        at += count
    run()
    for k in range(RHS):
        out[k : k + 1, :] = jnp.sum(acc[k], axis=0, keepdims=True)
    off = off_of()

    @pl.when((off >= 0) & (off < blocks))
    def _():
        for j in range(own_blocks):
            lane = pl.multiple_of(lax.bitwise_xor(off + j, flip) * nb, LANES)
            t = v[:, pl.ds(lane, nb)]
            cols = slice(j * nb, (j + 1) * nb)
            out[0:RHS, cols] = out[0:RHS, cols] + t[3:4] * t[0:RHS]
            out[RHS : 2 * RHS, cols] = t[0:RHS]


def cols_kernel(geo, peers, *refs):
    (nb, blocks, own_blocks, tiles, per_block, counts, total, flip_of, off_of) = geo
    n_keep = sum(1 for c in counts if c)
    s_hbm, *rest = refs
    keeps = rest[:n_keep]
    parts = rest[n_keep : n_keep + peers]
    even, odd, ring, w, wb, p0, p1, zs, sem = rest[n_keep + peers :]
    flip = flip_of()
    first = sum(counts)

    def finish(part, at):
        cols_finish(part, zs, at // nb, lax.rem(at, nb))

    def visit(src, row, chunk):
        at = chunk * CH
        finish(p1, jnp.maximum(at - BL, 0))
        cols_block(src, row, wb, p0, tiles)
        finish(p0, at)
        cols_block(src, row + BL, wb, p1, tiles)

    start, run = stream(
        s_hbm, ring, sem, None, None, first, 0, total, flip, per_block, visit
    )
    start()
    everything = parts[0][...]
    for part in parts[1:]:
        everything = everything + part[...]
    w[...] = everything
    for k in range(RHS):
        for c in range(tiles):
            wb[k * tiles + c] = jnp.broadcast_to(
                w[k : k + 1, c * LANES : (c + 1) * LANES], (SUB, LANES)
            )
    p1[...] = jnp.zeros_like(p1)
    zs[...] = jnp.zeros_like(zs)
    at = 0
    for ref, count in zip(keeps, [c for c in counts if c]):

        def step(i, _, ref=ref, at=at):
            visit(ref, i * CH, at + i)
            return 0

        lax.fori_loop(0, count, step, 0)
        at += count
    run()
    finish(p1, jnp.int32(total * CH - BL))
    off = off_of()

    @pl.when((off >= 0) & (off < blocks))
    def _():
        for j in range(own_blocks):
            at = lax.bitwise_xor(off + j, flip)
            zs[at, RHS : 2 * RHS, :] = w[0:RHS, j * nb : (j + 1) * nb]

    lane = lax.broadcasted_iota(jnp.int32, (1, LANES), 1)
    sums = jnp.zeros((1, LANES), jnp.float32)
    for k in range(RHS):
        b = w[RHS + k : RHS + k + 1, :]
        squares = jnp.sum(b * b, axis=1, keepdims=True)
        products = jnp.sum(b * w[k : k + 1, :], axis=1, keepdims=True)
        sums = sums + jnp.where(lane == k, squares, 0.0)
        sums = sums + jnp.where(lane == RHS + k, products, 0.0)
    for m in range(blocks):
        zs[m, 6:7, 0:LANES] = sums
    for t in range(blocks // 2):
        even[t] = zs[2 * t]
        odd[t] = zs[2 * t + 1]


def add_kernel(a, b, *outs):
    for t, out in enumerate(outs):
        out[...] = a[t] + b[t]


def pick(row, index):
    lane = lax.broadcasted_iota(jnp.int32, row.shape, 1)
    return jnp.sum(jnp.where(lane == index, row, 0.0), axis=1, keepdims=True)


def first_step_kernel(count, *refs):
    parts, (right, width, step, sums) = refs[:count], refs[count:]
    total = parts[0][...]
    for part in parts[1:]:
        total = total + part[...]
    lane = lax.broadcasted_iota(jnp.int32, (1, LANES), 1)
    head = total[6:7, 0:LANES]
    out = jnp.zeros((1, LANES), jnp.float32)
    for k in range(RHS):
        b = right[k : k + 1, :]
        w = total[RHS + k : RHS + k + 1, :]
        z = total[k : k + 1, :] + width[...] * w
        size = pick(head, k) / pick(head, RHS + k)
        residual = b - size * w
        image = w - size * z
        step[k : k + 1, :] = residual
        step[RHS + k : RHS + k + 1, :] = image
        step[8 + k : 9 + k, :] = w
        square = jnp.sum(residual * residual, axis=1, keepdims=True)
        product = jnp.sum(residual * image, axis=1, keepdims=True)
        out = out + jnp.where(lane == k, square, 0.0)
        out = out + jnp.where(lane == RHS + k, product, 0.0)
    step[6:7, :] = total[6:7, :]
    step[7:8, :] = jnp.zeros_like(step[7:8, :])
    step[8 + RHS :, :] = jnp.zeros_like(step[8 + RHS :, :])
    sums[...] = jnp.broadcast_to(out[None], sums.shape)


def second_step_kernel(step, sums, right, solution, residual):
    totals = jnp.sum(sums[...], axis=0)
    head = step[6:7, 0:LANES]
    for k in range(RHS):
        b = right[k : k + 1, :]
        r1 = step[k : k + 1, :]
        image = step[RHS + k : RHS + k + 1, :]
        norm0 = pick(head, k)
        size0 = norm0 / pick(head, RHS + k)
        norm1 = pick(totals, k)
        factor = norm1 / norm0
        size1 = norm1 / (pick(totals, RHS + k) - factor * norm1 / size0)
        w = step[8 + k : 9 + k, :]
        solution[k : k + 1, :] = size0 * b + size1 * (r1 + factor * b)
        residual[k : k + 1, :] = r1 - size1 * (image + factor * w)


def solution(mesh):
    rows, cols = mesh.shape["row"], mesh.shape["col"]
    devices = rows * cols

    def flips(s):
        return [(i, i ^ s) for i in range(cols)]

    def body(right_side, linewidth, scattering):
        n = right_side.shape[1]
        nr, nc = scattering.shape
        fast = n % CH == 0 and cols & (cols - 1) == 0 and cols > 1
        nb = n if fast else nc
        blocks, own_blocks = nr // nb, nc // nb
        tiles = nc // LANES
        total = nr // CH
        per_block = nb // CH

        def flip_of():
            return lax.axis_index("col") if fast else jnp.int32(0)

        def off_of():
            return lax.axis_index("col") * own_blocks - lax.axis_index("row") * blocks

        counts = [FIRST, SECOND, THIRD] if fast else [0, 0, 0]
        f32 = jnp.float32
        shape = jax.ShapeDtypeStruct

        def prefetch(first, count, after):
            return call(
                functools.partial(prefetch_kernel, first, count, flip_of, per_block),
                "prefetch",
                pltpu.VMEM((count * CH, nc), f32),
                1,
                ["hbm", "hbm"],
                [pltpu.SemaphoreType.DMA((count,))],
            )(scattering, after)

        packed = jnp.concatenate([right_side, linewidth[None]], axis=0)
        keeps = []
        if fast:
            other = lax.ppermute(packed, "col", flips(1))
            keeps.append(prefetch(0, counts[0], right_side))
            pair = call(merge_kernel, "merge", shape((8, n), f32), 1, ["", ""])(
                packed, other
            )
            pieces = [pair] + [
                lax.ppermute(pair, "col", flips(s)) for s in range(2, cols, 2)
            ]
            keeps.append(prefetch(counts[0], counts[1], pair))
        else:
            g = lax.all_gather(packed, "col", axis=1, tiled=True)
            g = g.reshape(4, blocks // 2, 2, nb).transpose(1, 2, 0, 3)
            pieces = [g[i].reshape(8, nb) for i in range(blocks // 2)]

        geo = (nb, blocks, own_blocks, tiles, per_block, counts, total, flip_of, off_of)
        scratch = [pltpu.VMEM((SLOTS, CH, nc), f32), pltpu.VMEM((RHS, SUB, nc), f32)]
        scratch += [pltpu.VMEM((RHS, BL, LANES), f32)] * 2 + [pltpu.VMEM((8, nr), f32)]
        out = [shape((8, nc), f32)]
        if counts[2]:
            out.append(pltpu.VMEM((counts[2] * CH, nc), f32))
            scratch.append(pltpu.SemaphoreType.DMA((counts[2],)))
        scratch.append(pltpu.SemaphoreType.DMA((SLOTS,)))
        image, *kept = call(
            functools.partial(rows_kernel, geo),
            "rows_product",
            out,
            20,
            ["hbm"] + [""] * (len(keeps) + len(pieces)),
            scratch,
        )(scattering, *[on_chip(k) for k in keeps], *pieces)
        keeps = keeps + kept
        parts = [image] + [
            lax.ppermute(image, "row", [(i, (i + s) % rows) for i in range(rows)])
            for s in range(1, rows)
        ]
        even, odd = call(
            functools.partial(cols_kernel, geo, len(parts)),
            "cols_product",
            [shape((blocks // 2, 8, nb), f32)] * 2,
            20,
            ["hbm"] + [""] * (len(keeps) + len(parts)),
            [
                pltpu.VMEM((SLOTS, CH, nc), f32),
                pltpu.VMEM((8, nc), f32),
                pltpu.VMEM((RHS * tiles, SUB, LANES), f32),
                pltpu.VMEM((RHS, BL, LANES), f32),
                pltpu.VMEM((RHS, BL, LANES), f32),
                pltpu.VMEM((blocks, 8, nb), f32),
                pltpu.SemaphoreType.DMA((SLOTS,)),
            ],
        )(scattering, *[on_chip(k) for k in keeps], *parts)
        if fast:
            came = lax.ppermute(odd, "col", flips(1))
            sums = call(
                add_kernel,
                "pair_sum",
                [shape((8, n), f32)] * (blocks // 2),
                4,
                ["", ""],
            )(even, came)
            chunks = [sums[0]] + [
                lax.ppermute(sums[t], "col", flips(2 * t)) for t in range(1, blocks // 2)
            ]
        else:
            whole = jnp.stack([even, odd], 1).reshape(blocks, 8, nb)
            heads = lax.psum(whole[0, 6, :LANES], "col")
            whole = whole.transpose(1, 0, 2).reshape(8, nr)
            chunk = lax.psum_scatter(whole, "col", scatter_dimension=1, tiled=True)
            chunks = [chunk.at[6, :LANES].set(heads)]
        step, message = call(
            functools.partial(first_step_kernel, len(chunks)),
            "first_step",
            [shape((16, n), f32), shape((devices, 1, LANES), f32)],
            4,
            [""] * (len(chunks) + 2),
        )(*chunks, right_side, linewidth[None])
        sums = lax.all_to_all(message, ("row", "col"), 0, 0, tiled=True)
        return tuple(
            call(
                second_step_kernel,
                "second_step",
                [shape((RHS, n), f32)] * 2,
                4,
                ["", "", ""],
            )(step, sums, right_side)
        )

    placed = (P(None, ("row", "col")), P(("row", "col")), P("row", "col"))
    return jax.shard_map(
        body,
        mesh=mesh,
        in_specs=placed,
        out_specs=(P(None, ("row", "col")), P(None, ("row", "col"))),
        check_vma=False,
    )
```

time: 396 us -> 101 us (0.26)
  blocking collectives: 166 us -> 9.51 us
  matrix products: 128 us -> 0 us
  waiting for transfers between devices: 84.7 us -> 14.1 us
  Pallas kernels: 0 us -> 57.5 us
  starting transfers between devices: 0.08 us -> 13.6 us
  between operations: 14.1 us -> 0.75 us
    unnamed x2 -> x0, matrix products: 128 us -> none
    all_gather x2 -> x0, blocking collectives: 87 us -> none  [apply_operator(): gathered = lax.all_gather(vectors, ('row', 'col'), axis=1, tiled=True)]
    unnamed x4 -> x0, waiting for transfers between devices: 84.7 us -> none
    psum x2 -> x0, blocking collectives: 78.6 us -> none  [two_products(): lax.psum((jnp.sum(residual * residual, axis=1), jnp.sum(residual * image,...]
    pallas_call x0 -> x8, Pallas kernels: none -> 57.5 us  [the longest x1 26.1 us: body(): call(functools.partial(rows_kernel, geo), 'rows_product', out, 20, ['hbm'...]
    ppermute x0 -> x11, waiting for transfers between devices: none -> 14.1 us  [the longest x3 7.54 us: body(): lax.ppermute(image, 'row', [(i, (i + s) % rows) for i in range(rows)])]
    ppermute x0 -> x11, starting transfers between devices: none -> 13.6 us  [the longest x3 5.05 us: body(): lax.ppermute(image, 'row', [(i, (i + s) % rows) for i in range(rows)])]
    all_to_all x0 -> x1, blocking collectives: none -> 9.51 us  [body(): sums = lax.all_to_all(message, ('row', 'col'), 0, 0, tiled=True)]
  transfers between devices with their start and end apart: 2 -> 11, of which waited for: 2 -> 7; matrix products, arithmetic and copies ran while one was open for 0% -> 0% of each run, Pallas kernels for 0% -> 10%
where the time goes in v1:
time: 101 us; the launch traced here: 100 us
  Pallas kernels  57.5 us (57%)
  waiting for transfers between devices  14.1 us (14%)
  starting transfers between devices  13.6 us (13%)
  blocking collectives  9.51 us (9%)
  local copies, waits for them, and re-layouts  4.19 us (4%)
    pallas_call x1, Pallas kernels, body(): call(functools.partial(rows_kernel, geo), 'rows_product', out, 20, ['hbm'...  26.1 us
    pallas_call x1, Pallas kernels, body(): call(functools.partial(cols_kernel, geo, len(parts)), 'cols_product', [sh...  20.2 us
    pallas_call x2, Pallas kernels, prefetch(): call(functools.partial(prefetch_kernel, first, count, flip_of, per_block)...  10.3 us
    all_to_all x1, blocking collectives, body(): sums = lax.all_to_all(message, ('row', 'col'), 0, 0, tiled=True)  9.51 us
    ppermute x3, waiting for transfers between devices, body(): lax.ppermute(image, 'row', [(i, (i + s) % rows) for i in range(rows)])  7.54 us
    ppermute x3, starting transfers between devices, body(): lax.ppermute(image, 'row', [(i, (i + s) % rows) for i in range(rows)])  5.05 us
    ppermute x3, starting transfers between devices, body(): lax.ppermute(pair, 'col', flips(s))  4.41 us
    ppermute x3, waiting for transfers between devices, body(): lax.ppermute(sums[t], 'col', flips(2 * t))  4.24 us
  transfers between devices with their start and end apart: 11, of which 7 were waited for; matrix products, arithmetic and copies ran while one was open for 0% of the time, Pallas kernels for 10%

profile of v1, /device:TPU:0, one launch (start us, length us, event | category | flops | bytes accessed | tf_op | source)
XLA Modules:
  0.0 100.5 jit_solution(14088675922561599702)
XLA Ops:
  0.6 0.7 broadcast_in_dim.4.refs_5_
  1.3 0.7 pad_maximum_fusion.a
  2.6 0.8 collective-permute-done.b
  3.4 3.8 %collective-permute-start.3 = (f32[8,768]{1,0:T(8,128)S(1)}, f32[8,768]{1,0:T(8,128)S(1)}, u32[]{:S(2)}, u32[]{:S(2)}) collective-permute-start(f32[8,768]{1,0:T(8,128)S(1)} %merge.1.after.refs_3_), channel_id=1, source_target_pairs={{0,6},{1,7},{2,4},{3,5},{4,2},{5,3},{6,0},{7,1},{8,14},{9,15},{10,... | collective-permute-start | bytes 73736 | tf_op jit(solution)/shard_map/ppermute | solution.py:399
  7.9 0.7 copy-done.1
  8.6 3.8 %prefetch.2.refs_1_ = f32[768,3072]{1,0:T(8,128)S(1)} custom-call(f32[6144,3072]{1,0:T(8,128)} %refs_0_.3, f32[3,768]{1,0:T(4,128)S(1)} %copy-done.1), custom_call_target="tpu_custom_call" | custom-call | tf_op jit(solution)/shard_map/prefetch/pallas_call | solution.py:381
  12.4 6.5 %prefetch.3.refs_2_ = f32[1536,3072]{1,0:T(8,128)S(1)} custom-call(f32[6144,3072]{1,0:T(8,128)} %refs_0_.3, f32[8,768]{1,0:T(8,128)S(1)} %merge.1.after.refs_3_), custom_call_target="tpu_custom_call" | custom-call | tf_op jit(solution)/shard_map/prefetch/pallas_call | solution.py:381
  18.9 0.6 copy-done.7
  19.5 0.6 copy-done.9
  20.1 26.1 %rows_product.1 = (f32[8,3072]{1,0:T(8,128)}, f32[1280,3072]{1,0:T(8,128)S(1)}) custom-call(f32[6144,3072]{1,0:T(8,128)} %refs_0_.3, f32[768,3072]{1,0:T(8,128)S(1)} %prefetch.2.refs_1_, f32[1536,3072]{1,0:T(8,128)S(1)} %prefetch.3.refs_2_, f32[8,768]{1,0:T(8,128)} %copy-done, f32[8,768]{1,0:T(8,128)} %copy-done.9, f32[8,768]{1,0:T(8,128)} %copy-done.8, ...), custom_call_target="tpu_custom_call" | custom-call | tf_op jit(solution)/shard_map/rows_product/pallas_call | solution.py:415
  46.2 4.0 %collective-permute-start.6 = (f32[8,3072]{1,0:T(8,128)}, f32[8,3072]{1,0:T(8,128)S(1)}, u32[]{:S(2)}, u32[]{:S(2)}) collective-permute-start(f32[8,3072]{1,0:T(8,128)} %get-tuple-element.13.refs_4_), channel_id=1, source_target_pairs={{0,24},{8,0},{16,8},{24,16},{1,25},{9,1},{17,9},{25,17},{2,26},{10... | collective-permute-start | bytes 294920 | tf_op jit(solution)/shard_map/ppermute | solution.py:425
  50.3 1.0 %collective-permute-start.4 = (f32[8,3072]{1,0:T(8,128)}, f32[8,3072]{1,0:T(8,128)S(1)}, u32[]{:S(2)}, u32[]{:S(2)}) collective-permute-start(f32[8,3072]{1,0:T(8,128)} %get-tuple-element.13.refs_4_), channel_id=1, source_target_pairs={{0,8},{8,16},{16,24},{24,0},{1,9},{9,17},{17,25},{25,1},{2,10},{10... | collective-permute-start | bytes 294920 | tf_op jit(solution)/shard_map/ppermute | solution.py:425
  51.3 2.5 %collective-permute-done.6.refs_7_ = f32[8,3072]{1,0:T(8,128)S(1)} collective-permute-done((f32[8,3072]{1,0:T(8,128)}, f32[8,3072]{1,0:T(8,128)S(1)}, u32[]{:S(2)}, u32[]{:S(2)}) %collective-permute-start.6) | collective-permute-done | bytes 98336 | tf_op jit(solution)/shard_map/ppermute | solution.py:425
  53.8 5.1 %collective-permute-done.5.refs_6_ = f32[8,3072]{1,0:T(8,128)S(1)} collective-permute-done((f32[8,3072]{1,0:T(8,128)}, f32[8,3072]{1,0:T(8,128)S(1)}, u32[]{:S(2)}, u32[]{:S(2)}) %collective-permute-start.5) | collective-permute-done | bytes 98336 | tf_op jit(solution)/shard_map/ppermute | solution.py:425
  58.8 0.6 copy-done.5
  59.5 20.2 %cols_product.1 = (f32[4,8,768]{2,1,0:T(8,128)}, f32[4,8,768]{2,1,0:T(8,128)}) custom-call(f32[6144,3072]{1,0:T(8,128)} %refs_0_.3, f32[768,3072]{1,0:T(8,128)S(1)} %prefetch.2.refs_1_, f32[1536,3072]{1,0:T(8,128)S(1)} %prefetch.3.refs_2_, f32[1280,3072]{1,0:T(8,128)S(1)} %get-tuple-element.12.refs_3_, f32[8,3072]{1,0:T(8,128)} %get-tuple-element.13.refs_4_, ...), custom_call_target="tpu_custom_call" | custom-call | tf_op jit(solution)/shard_map/cols_product/pallas_call | solution.py:428
  79.8 1.5 %collective-permute-done.7.b = f32[4,8,768]{2,1,0:T(8,128)S(1)} collective-permute-done((f32[4,8,768]{2,1,0:T(8,128)}, f32[4,8,768]{2,1,0:T(8,128)S(1)}, u32[]{:S(2)}, u32[]{:S(2)}) %collective-permute-start.7) | collective-permute-done | bytes 98336 | tf_op jit(solution)/shard_map/ppermute | solution.py:445
  81.3 0.9 copy-done.3
  82.2 1.6 %collective-permute-start.8 = (f32[8,768]{1,0:T(8,128)S(1)}, f32[8,768]{1,0:T(8,128)S(1)}, u32[]{:S(2)}, u32[]{:S(2)}) collective-permute-start(f32[8,768]{1,0:T(8,128)S(1)} %get-tuple-element.17), channel_id=1, source_target_pairs={{0,2},{1,3},{2,0},{3,1},{4,6},{5,7},{6,4},{7,5},{8,10},{9,11},{10,... | collective-permute-start | bytes 73736 | tf_op jit(solution)/shard_map/ppermute | solution.py:454
  83.7 1.5 %collective-permute-start.9 = (f32[8,768]{1,0:T(8,128)S(1)}, f32[8,768]{1,0:T(8,128)S(1)}, u32[]{:S(2)}, u32[]{:S(2)}) collective-permute-start(f32[8,768]{1,0:T(8,128)S(1)} %get-tuple-element.18), channel_id=1, source_target_pairs={{0,4},{1,5},{2,6},{3,7},{4,0},{5,1},{6,2},{7,3},{8,12},{9,13},{10,... | collective-permute-start | bytes 73736 | tf_op jit(solution)/shard_map/ppermute | solution.py:454
  86.1 1.5 %collective-permute-done.9.refs_2_ = f32[8,768]{1,0:T(8,128)S(1)} collective-permute-done((f32[8,768]{1,0:T(8,128)S(1)}, f32[8,768]{1,0:T(8,128)S(1)}, u32[]{:S(2)}, u32[]{:S(2)}) %collective-permute-start.9) | collective-permute-done | bytes 24608 | tf_op jit(solution)/shard_map/ppermute | solution.py:454
  87.6 2.4 %collective-permute-done.10.refs_3_ = f32[8,768]{1,0:T(8,128)S(1)} collective-permute-done((f32[8,768]{1,0:T(8,128)S(1)}, f32[8,768]{1,0:T(8,128)S(1)}, u32[]{:S(2)}, u32[]{:S(2)}) %collective-permute-start.10) | collective-permute-done | bytes 24608 | tf_op jit(solution)/shard_map/ppermute | solution.py:454
  90.2 9.5 %all_to_all.5.sums = f32[32,1,128]{2,1,0:T(1,128)S(1)} all-to-all(f32[32,1,128]{2,1,0:T(1,128)S(1)} %get-tuple-element.21), channel_id=1, replica_groups=mesh['row'=4,'col'=8] {'row','col'}, dimensions={0} | all-to-all | bytes 32768 | tf_op jit(solution)/shard_map/all_to_all | solution.py:469
  99.7 0.8 second_step.1
  (29 shorter events, 2.4 us)
Async XLA Ops:
  2.0 1.4 %collective-permute-start = (f32[4,768]{1,0:T(4,128)S(1)}, f32[4,768]{1,0:T(4,128)S(1)}, u32[]{:S(2)}, u32[]{:S(2)}) collective-permute-start(f32[4,768]{1,0:T(4,128)S(1)} %pad_maximum_fusion.a), channel_id=1, source_target_pairs={{0,1},{1,0},{2,3},{3,2},{4,5},{5,4},{6,7},{7,6},{8,9},{9,8},{10,11... | collective-permute-start | bytes 36872 | tf_op jit(solution)/shard_map/ppermute | solution.py:393
  3.4 8.9 %copy-start = (f32[8,768]{1,0:T(8,128)}, f32[8,768]{1,0:T(8,128)S(1)}, u32[]{:S(2)}) copy-start(f32[8,768]{1,0:T(8,128)S(1)} %merge.1.after.refs_3_) | copy-start | bytes 73732
  3.4 15.4 %collective-permute-start.3 = (f32[8,768]{1,0:T(8,128)S(1)}, f32[8,768]{1,0:T(8,128)S(1)}, u32[]{:S(2)}, u32[]{:S(2)}) collective-permute-start(f32[8,768]{1,0:T(8,128)S(1)} %merge.1.after.refs_3_), channel_id=1, source_target_pairs={{0,6},{1,7},{2,4},{3,5},{4,2},{5,3},{6,0},{7,1},{8,14},{9,15},{10,... | collective-permute-start | bytes 73736 | tf_op jit(solution)/shard_map/ppermute | solution.py:399
  7.2 11.7 %collective-permute-start.2 = (f32[8,768]{1,0:T(8,128)S(1)}, f32[8,768]{1,0:T(8,128)S(1)}, u32[]{:S(2)}, u32[]{:S(2)}) collective-permute-start(f32[8,768]{1,0:T(8,128)S(1)} %merge.1.after.refs_3_), channel_id=1, source_target_pairs={{0,4},{1,5},{2,6},{3,7},{4,0},{5,1},{6,2},{7,3},{8,12},{9,13},{10,... | collective-permute-start | bytes 73736 | tf_op jit(solution)/shard_map/ppermute | solution.py:399
  7.7 11.2 %collective-permute-start.1 = (f32[8,768]{1,0:T(8,128)S(1)}, f32[8,768]{1,0:T(8,128)S(1)}, u32[]{:S(2)}, u32[]{:S(2)}) collective-permute-start(f32[8,768]{1,0:T(8,128)S(1)} %merge.1.after.refs_3_), channel_id=1, source_target_pairs={{0,2},{1,3},{2,0},{3,1},{4,6},{5,7},{6,4},{7,5},{8,10},{9,11},{10,... | collective-permute-start | bytes 73736 | tf_op jit(solution)/shard_map/ppermute | solution.py:399
  7.9 0.7 copy-start.1
  18.9 0.6 copy-start.7
  18.9 0.6 copy-start.8
  19.5 0.6 copy-start.9
  46.2 7.5 %collective-permute-start.6 = (f32[8,3072]{1,0:T(8,128)}, f32[8,3072]{1,0:T(8,128)S(1)}, u32[]{:S(2)}, u32[]{:S(2)}) collective-permute-start(f32[8,3072]{1,0:T(8,128)} %get-tuple-element.13.refs_4_), channel_id=1, source_target_pairs={{0,24},{8,0},{16,8},{24,16},{1,25},{9,1},{17,9},{25,17},{2,26},{10... | collective-permute-start | bytes 294920 | tf_op jit(solution)/shard_map/ppermute | solution.py:425
  50.3 8.6 %collective-permute-start.5 = (f32[8,3072]{1,0:T(8,128)}, f32[8,3072]{1,0:T(8,128)S(1)}, u32[]{:S(2)}, u32[]{:S(2)}) collective-permute-start(f32[8,3072]{1,0:T(8,128)} %get-tuple-element.13.refs_4_), channel_id=1, source_target_pairs={{0,16},{8,24},{16,0},{24,8},{1,17},{9,25},{17,1},{25,9},{2,18},{10... | collective-permute-start | bytes 294920 | tf_op jit(solution)/shard_map/ppermute | solution.py:425
  50.3 8.6 %collective-permute-start.4 = (f32[8,3072]{1,0:T(8,128)}, f32[8,3072]{1,0:T(8,128)S(1)}, u32[]{:S(2)}, u32[]{:S(2)}) collective-permute-start(f32[8,3072]{1,0:T(8,128)} %get-tuple-element.13.refs_4_), channel_id=1, source_target_pairs={{0,8},{8,16},{16,24},{24,0},{1,9},{9,17},{17,25},{25,1},{2,10},{10... | collective-permute-start | bytes 294920 | tf_op jit(solution)/shard_map/ppermute | solution.py:425
  53.8 5.1 %copy-start.4 = (f32[8,3072]{1,0:T(8,128)}, f32[8,3072]{1,0:T(8,128)S(1)}, u32[]{:S(2)}) copy-start(f32[8,3072]{1,0:T(8,128)S(1)} %collective-permute-done.6.refs_7_) | copy-start | bytes 294916
  58.8 0.6 copy-start.5
  58.8 0.7 copy-start.6
  59.5 30.5 %copy-start.2 = (f32[3,768]{1,0:T(4,128)S(1)}, f32[3,768]{1,0:T(4,128)}, u32[]{:S(2)}) copy-start(f32[3,768]{1,0:T(4,128)} %right.1) | copy-start | bytes 27652
  79.7 1.6 %collective-permute-start.7 = (f32[4,8,768]{2,1,0:T(8,128)}, f32[4,8,768]{2,1,0:T(8,128)S(1)}, u32[]{:S(2)}, u32[]{:S(2)}) collective-permute-start(f32[4,8,768]{2,1,0:T(8,128)} %get-tuple-element.15), channel_id=1, source_target_pairs={{0,1},{1,0},{2,3},{3,2},{4,5},{5,4},{6,7},{7,6},{8,9},{9,8},{10,11... | collective-permute-start | bytes 294920 | tf_op jit(solution)/shard_map/ppermute | solution.py:445
  81.3 0.9 copy-start.3
  82.2 3.9 %collective-permute-start.8 = (f32[8,768]{1,0:T(8,128)S(1)}, f32[8,768]{1,0:T(8,128)S(1)}, u32[]{:S(2)}, u32[]{:S(2)}) collective-permute-start(f32[8,768]{1,0:T(8,128)S(1)} %get-tuple-element.17), channel_id=1, source_target_pairs={{0,2},{1,3},{2,0},{3,1},{4,6},{5,7},{6,4},{7,5},{8,10},{9,11},{10,... | collective-permute-start | bytes 73736 | tf_op jit(solution)/shard_map/ppermute | solution.py:454
  83.7 3.8 %collective-permute-start.9 = (f32[8,768]{1,0:T(8,128)S(1)}, f32[8,768]{1,0:T(8,128)S(1)}, u32[]{:S(2)}, u32[]{:S(2)}) collective-permute-start(f32[8,768]{1,0:T(8,128)S(1)} %get-tuple-element.18), channel_id=1, source_target_pairs={{0,4},{1,5},{2,6},{3,7},{4,0},{5,1},{6,2},{7,3},{8,12},{9,13},{10,... | collective-permute-start | bytes 73736 | tf_op jit(solution)/shard_map/ppermute | solution.py:454
  85.2 4.7 %collective-permute-start.10 = (f32[8,768]{1,0:T(8,128)S(1)}, f32[8,768]{1,0:T(8,128)S(1)}, u32[]{:S(2)}, u32[]{:S(2)}) collective-permute-start(f32[8,768]{1,0:T(8,128)S(1)} %get-tuple-element.19), channel_id=1, source_target_pairs={{0,6},{1,7},{2,4},{3,5},{4,2},{5,3},{6,0},{7,1},{8,14},{9,15},{10,... | collective-permute-start | bytes 73736 | tf_op jit(solution)/shard_map/ppermute | solution.py:454

commit v2 on v1

--- a/solution.py
+++ b/solution.py
@@ -11,12 +11,15 @@
 SUB = 8
 BL = 128
 CH = 256
+GROUP = 8
 RHS = 3
-FIRST = 3
-SECOND = 6
-THIRD = 5
+FIRST = 2
+THIRD = 6
+STAY = 6
 SLOTS = 4
 AHEAD = 4
+UNROLL = 4
+GRANT = 16
 
 HBM = pl.BlockSpec(memory_space=pltpu.HBM)
 VMEM = pl.BlockSpec(memory_space=pltpu.VMEM)
@@ -44,11 +47,16 @@
     )
 
 
-def prefetch_kernel(first, count, flip_of, per_block, s_hbm, after, keep, sem):
+def pack_kernel(right, width, out):
+    out[0:RHS, :] = right[...]
+    out[RHS : RHS + 1, :] = width[...].reshape(1, width.shape[0])
+
+
+def prefetch_kernel(count, flip_of, per_block, s_hbm, after, keep, sem):
     flip = flip_of()
     copies = []
     for i in range(count):
-        row = row_of(jnp.int32(first + i), flip, per_block)
+        row = row_of(jnp.int32(i), flip, per_block)
         copies.append(
             pltpu.make_async_copy(
                 s_hbm.at[pl.ds(row, CH)], keep.at[pl.ds(i * CH, CH)], sem.at[i]
@@ -64,28 +72,34 @@
     out[4:8, :] = b[...]
 
 
-def spread(v, vb, start):
-    t = jnp.transpose(v[:, pl.ds(pl.multiple_of(start, BL), BL)])
-    for k in range(RHS):
-        vb[k] = jnp.broadcast_to(t[:, k : k + 1], (BL, LANES))
-
-
-def rows_block(src, row, vb, acc, tiles, v, next_vb, next_start):
-    half = tiles // 2
-    for h in range(0, tiles, half):
-        cols = [slice(c * LANES, (c + 1) * LANES) for c in range(h, h + half)]
-        a = [[acc[k, :, c] for c in cols] for k in range(RHS)]
+def spread(v, vb, start, rows):
+    def one(at):
+        t = jnp.transpose(v[:, pl.ds(pl.multiple_of(start + at, BL), BL)])
+        for k in range(RHS):
+            vb[k, pl.ds(pl.multiple_of(at, BL), BL), :] = jnp.broadcast_to(
+                t[:, k : k + 1], (BL, LANES)
+            )
+
+    def step(i, _):
+        for u in range(UNROLL):
+            one(i * (UNROLL * BL) + u * BL)
+        return 0
+
+    lax.fori_loop(0, rows // (UNROLL * BL), step, 0)
+
+
+def rows_block(src, row, vb, at, acc, tiles):
+    for h in range(0, tiles, GROUP):
+        width = min(GROUP, tiles - h)
+        cols = slice(h * LANES, (h + width) * LANES)
+        a = [acc[k, :, cols] for k in range(RHS)]
         for g in range(BL // SUB):
-            b = [vb[k, g * SUB : (g + 1) * SUB, :] for k in range(RHS)]
-            for j, c in enumerate(cols):
-                t = src[pl.ds(row + g * SUB, SUB), c]
-                for k in range(RHS):
-                    a[k][j] = a[k][j] + t * b[k]
+            t = src[pl.ds(row + g * SUB, SUB), cols]
+            for k in range(RHS):
+                b = vb[k, pl.ds(pl.multiple_of(at + g * SUB, SUB), SUB), :]
+                a[k] = a[k] + t * jnp.concatenate([b] * width, axis=1)
         for k in range(RHS):
-            for j, c in enumerate(cols):
-                acc[k, :, c] = a[k][j]
-        if h == 0:
-            spread(v, next_vb, next_start)
+            acc[k, :, cols] = a[k]
 
 
 def cols_block(src, row, wb, part, tiles):
@@ -107,11 +121,11 @@
         zs[block, k : k + 1, pl.ds(pl.multiple_of(lane, BL), BL)] = total
 
 
-def stream(s_hbm, ring, sem, keep, keep_sem, first, kept, total, flip, per_block, visit):
+def stream(s_hbm, ring, sem, keep, keep_sem, first, kept, total, flip, per_block, visit, hi=None):
     def kept_copy(i):
         return pltpu.make_async_copy(
             s_hbm.at[pl.ds(row_of(first + i, flip, per_block), CH)],
-            keep.at[pl.ds(pl.multiple_of(i * CH, CH), CH)],
+            keep.at[pl.ds(pl.multiple_of((first + i) * CH, CH), CH)],
             keep_sem.at[i],
         )
 
@@ -148,7 +162,14 @@
                 def _():
                     ring_copy(ahead).start()
 
-            visit(keep, i * CH, first + i)
+            if hi is None or hi >= first + kept:
+                visit(keep, (first + i) * CH, first + i)
+            else:
+
+                @pl.when(first + i < hi)
+                def _():
+                    visit(keep, (first + i) * CH, first + i)
+
             return 0
 
         if kept:
@@ -170,48 +191,62 @@
     return start, run
 
 
-def rows_kernel(geo, *refs):
-    (nb, blocks, own_blocks, tiles, per_block, counts, total, flip_of, off_of) = geo
-    n_keep = sum(1 for c in counts[:2] if c)
+def rows_kernel(geo, lo, hi, have, stay, split, *refs):
+    (nb, blocks, own_blocks, tiles, per_block, total, flip_of, off_of) = geo
     s_hbm, *rest = refs
-    keeps = rest[:n_keep]
-    pieces = rest[n_keep : n_keep + blocks // 2]
-    rest = rest[n_keep + blocks // 2 :]
-    if counts[2]:
-        out, keep, ring, acc, vb0, vb1, v, keep_sem, sem = rest
+    count = (hi + 2 * per_block - 1) // (2 * per_block)
+    pieces, rest = rest[:count], rest[count:]
+    before = keep = keep_sem = ring = sem = None
+    if lo:
+        before, *rest = rest
+    if have:
+        _, *rest = rest
+    out, *rest = rest
+    if stay:
+        keep, *rest = rest
+    if split:
+        acc = out
     else:
-        out, ring, acc, vb0, vb1, v, sem = rest
-        keep = keep_sem = None
+        acc, *rest = rest
+    vb, v, *rest = rest
+    if stay:
+        keep_sem, *rest = rest
+    ringed = max(0, hi - have - stay)
+    if ringed:
+        ring, sem = rest
     flip = flip_of()
-    first = counts[0] + counts[1]
+    pair = 2 * nb
 
     def visit(src, row, chunk):
-        at = chunk * CH
-        rows_block(src, row, vb0, acc, tiles, v, vb1, at + BL)
-        following = jnp.minimum(at + CH, (total - 1) * CH)
-        rows_block(src, row + BL, vb1, acc, tiles, v, vb0, following)
+        at = lax.rem(chunk * CH, pair)
+
+        @pl.when(at == 0)
+        def _():
+            spread(v, vb, chunk * CH, pair)
+
+        for u in range(0, CH, BL):
+            rows_block(src, row + u, vb, at + u, acc, tiles)
 
     start, run = stream(
-        s_hbm, ring, sem, keep, keep_sem, first, counts[2], total, flip, per_block, visit
+        s_hbm, ring, sem, keep, keep_sem, have, stay, have + stay + ringed, flip, per_block, visit, hi
     )
     start()
-    v[4:8, :] = jnp.zeros_like(v[4:8, :])
+    v[RHS + 1 :, :] = jnp.zeros_like(v[RHS + 1 :, :])
     for i, piece in enumerate(pieces):
         v[0:4, 2 * i * nb : (2 * i + 1) * nb] = piece[0:4, :]
         v[0:4, (2 * i + 1) * nb : (2 * i + 2) * nb] = piece[4:8, :]
-    acc[...] = jnp.zeros_like(acc)
+    acc[...] = before[...] if lo else jnp.zeros_like(acc)
+
+    def step(i, _):
+        visit(keep, i * CH, i)
+        return 0
+
+    if have > lo:
+        lax.fori_loop(lo, have, step, 0)
+    run()
+    if split:
+        return
     out[...] = jnp.zeros_like(out)
-    spread(v, vb0, jnp.int32(0))
-    at = 0
-    for ref, count in zip(keeps, [c for c in counts[:2] if c]):
-
-        def step(i, _, ref=ref, at=at):
-            visit(ref, i * CH, at + i)
-            return 0
-
-        lax.fori_loop(0, count, step, 0)
-        at += count
-    run()
     for k in range(RHS):
         out[k : k + 1, :] = jnp.sum(acc[k], axis=0, keepdims=True)
     off = off_of()
@@ -226,15 +261,15 @@
             out[RHS : 2 * RHS, cols] = t[0:RHS]
 
 
-def cols_kernel(geo, peers, *refs):
-    (nb, blocks, own_blocks, tiles, per_block, counts, total, flip_of, off_of) = geo
-    n_keep = sum(1 for c in counts if c)
+def cols_kernel(geo, first, peers, *refs):
+    (nb, blocks, own_blocks, tiles, per_block, total, flip_of, off_of) = geo
     s_hbm, *rest = refs
-    keeps = rest[:n_keep]
-    parts = rest[n_keep : n_keep + peers]
-    even, odd, ring, w, wb, p0, p1, zs, sem = rest[n_keep + peers :]
+    keep = None
+    if first:
+        keep, *rest = rest
+    parts, rest = rest[:peers], rest[peers:]
+    even, odd, ring, w, wb, p0, p1, zs, sem = rest
     flip = flip_of()
-    first = sum(counts)
 
     def finish(part, at):
         cols_finish(part, zs, at // nb, lax.rem(at, nb))
@@ -261,15 +296,13 @@
             )
     p1[...] = jnp.zeros_like(p1)
     zs[...] = jnp.zeros_like(zs)
-    at = 0
-    for ref, count in zip(keeps, [c for c in counts if c]):
-
-        def step(i, _, ref=ref, at=at):
-            visit(ref, i * CH, at + i)
-            return 0
-
-        lax.fori_loop(0, count, step, 0)
-        at += count
+
+    def step(i, _):
+        visit(keep, i * CH, i)
+        return 0
+
+    if first:
+        lax.fori_loop(0, first, step, 0)
     run()
     finish(p1, jnp.int32(total * CH - BL))
     off = off_of()
@@ -373,64 +406,87 @@
         def off_of():
             return lax.axis_index("col") * own_blocks - lax.axis_index("row") * blocks
 
-        counts = [FIRST, SECOND, THIRD] if fast else [0, 0, 0]
         f32 = jnp.float32
         shape = jax.ShapeDtypeStruct
 
-        def prefetch(first, count, after):
+        def small(dims):
+            return pltpu.VMEM(dims, f32) if fast else shape(dims, f32)
+
+        def near(x):
+            return on_chip(x) if fast else x
+
+        kept = pltpu.VMEM(((FIRST + THIRD + STAY) * CH, nc), f32)
+
+        geo = (nb, blocks, own_blocks, tiles, per_block, total, flip_of, off_of)
+
+        def rows_product(lo, hi, have, stay, operands, split, name):
+            out = [small((RHS, SUB, nc)) if split else shape((8, nc), f32)]
+            scratch = [] if split else [pltpu.VMEM((RHS, SUB, nc), f32)]
+            scratch += [pltpu.VMEM((RHS, 2 * nb, LANES), f32), pltpu.VMEM((8, nr), f32)]
+            if stay:
+                out.append(kept)
+                scratch.append(pltpu.SemaphoreType.DMA((stay,)))
+            if hi - have - stay > 0:
+                scratch.append(pltpu.VMEM((SLOTS, CH, nc), f32))
+                scratch.append(pltpu.SemaphoreType.DMA((SLOTS,)))
             return call(
-                functools.partial(prefetch_kernel, first, count, flip_of, per_block),
+                functools.partial(rows_kernel, geo, lo, hi, have, stay, split),
+                name,
+                out,
+                GRANT,
+                ["hbm"] + [""] * len(operands),
+                scratch,
+                input_output_aliases={len(operands): 1} if have else {},
+            )(scattering, *[near(x) for x in operands])
+
+        held = []
+        if fast:
+            packed = call(pack_kernel, "pack", small((4, n)), GRANT, ["", ""])(
+                right_side, linewidth
+            )
+            other = lax.ppermute(packed, "col", flips(1))
+            held = call(
+                functools.partial(prefetch_kernel, FIRST, flip_of, per_block),
                 "prefetch",
-                pltpu.VMEM((count * CH, nc), f32),
-                1,
-                ["hbm", "hbm"],
-                [pltpu.SemaphoreType.DMA((count,))],
-            )(scattering, after)
-
-        packed = jnp.concatenate([right_side, linewidth[None]], axis=0)
-        keeps = []
-        if fast:
-            other = lax.ppermute(packed, "col", flips(1))
-            keeps.append(prefetch(0, counts[0], right_side))
-            pair = call(merge_kernel, "merge", shape((8, n), f32), 1, ["", ""])(
-                packed, other
+                kept,
+                GRANT,
+                ["hbm", ""],
+                [pltpu.SemaphoreType.DMA((FIRST,))],
+            )(scattering, on_chip(packed))
+            pair = call(merge_kernel, "merge", small((8, n)), GRANT, ["", ""])(
+                on_chip(packed), on_chip(other)
             )
             pieces = [pair] + [
                 lax.ppermute(pair, "col", flips(s)) for s in range(2, cols, 2)
             ]
-            keeps.append(prefetch(counts[0], counts[1], pair))
+            middle = 2 * per_block
+            have = FIRST
+            begun, held = rows_product(
+                0, middle, have, THIRD, [pair, held], True, "rows_begin"
+            )
+            have += THIRD
+            image, held = rows_product(
+                middle, total, have, STAY, pieces + [begun, held], False, "rows_rest"
+            )
+            have += STAY
+            held = [held]
         else:
+            packed = jnp.concatenate([right_side, linewidth[None]], axis=0)
             g = lax.all_gather(packed, "col", axis=1, tiled=True)
             g = g.reshape(4, blocks // 2, 2, nb).transpose(1, 2, 0, 3)
             pieces = [g[i].reshape(8, nb) for i in range(blocks // 2)]
-
-        geo = (nb, blocks, own_blocks, tiles, per_block, counts, total, flip_of, off_of)
-        scratch = [pltpu.VMEM((SLOTS, CH, nc), f32), pltpu.VMEM((RHS, SUB, nc), f32)]
-        scratch += [pltpu.VMEM((RHS, BL, LANES), f32)] * 2 + [pltpu.VMEM((8, nr), f32)]
-        out = [shape((8, nc), f32)]
-        if counts[2]:
-            out.append(pltpu.VMEM((counts[2] * CH, nc), f32))
-            scratch.append(pltpu.SemaphoreType.DMA((counts[2],)))
-        scratch.append(pltpu.SemaphoreType.DMA((SLOTS,)))
-        image, *kept = call(
-            functools.partial(rows_kernel, geo),
-            "rows_product",
-            out,
-            20,
-            ["hbm"] + [""] * (len(keeps) + len(pieces)),
-            scratch,
-        )(scattering, *[on_chip(k) for k in keeps], *pieces)
-        keeps = keeps + kept
+            have = 0
+            (image,) = rows_product(0, total, 0, 0, pieces, False, "rows_product")
         parts = [image] + [
             lax.ppermute(image, "row", [(i, (i + s) % rows) for i in range(rows)])
             for s in range(1, rows)
         ]
         even, odd = call(
-            functools.partial(cols_kernel, geo, len(parts)),
+            functools.partial(cols_kernel, geo, have, len(parts)),
             "cols_product",
             [shape((blocks // 2, 8, nb), f32)] * 2,
-            20,
-            ["hbm"] + [""] * (len(keeps) + len(parts)),
+            GRANT,
+            ["hbm"] + [""] * (len(held) + len(parts)),
             [
                 pltpu.VMEM((SLOTS, CH, nc), f32),
                 pltpu.VMEM((8, nc), f32),
@@ -440,16 +496,16 @@
                 pltpu.VMEM((blocks, 8, nb), f32),
                 pltpu.SemaphoreType.DMA((SLOTS,)),
             ],
-        )(scattering, *[on_chip(k) for k in keeps], *parts)
+        )(scattering, *[on_chip(k) for k in held], *parts)
         if fast:
             came = lax.ppermute(odd, "col", flips(1))
             sums = call(
                 add_kernel,
                 "pair_sum",
-                [shape((8, n), f32)] * (blocks // 2),
+                [small((8, n))] * (blocks // 2),
                 4,
                 ["", ""],
-            )(even, came)
+            )(on_chip(even), on_chip(came))
             chunks = [sums[0]] + [
                 lax.ppermute(sums[t], "col", flips(2 * t)) for t in range(1, blocks // 2)
             ]
@@ -462,10 +518,10 @@
         step, message = call(
             functools.partial(first_step_kernel, len(chunks)),
             "first_step",
-            [shape((16, n), f32), shape((devices, 1, LANES), f32)],
+            [small((16, n)), small((devices, 1, LANES))],
             4,
             [""] * (len(chunks) + 2),
-        )(*chunks, right_side, linewidth[None])
+        )(*[near(c) for c in chunks], right_side, linewidth[None])
         sums = lax.all_to_all(message, ("row", "col"), 0, 0, tiled=True)
         return tuple(
             call(
@@ -474,7 +530,7 @@
                 [shape((RHS, n), f32)] * 2,
                 4,
                 ["", "", ""],
-            )(step, sums, right_side)
+            )(near(step), near(sums), right_side)
         )
 
     placed = (P(None, ("row", "col")), P(("row", "col")), P("row", "col"))

time: 101 us -> 92.9 us (0.920)
  Pallas kernels: 57.5 us -> 51.9 us
  waiting for transfers between devices: 14.1 us -> 10.7 us
  blocking collectives: 9.51 us -> 11.8 us
  local copies, waits for them, and re-layouts: 4.19 us -> 2.96 us
    pallas_call x7 -> x8, Pallas kernels: 56.8 us -> 51.1 us  [the longest x2 24.3 us: rows_product(): call(functools.partial(rows_kernel, geo, lo, hi, have, stay, split), name...]
    ppermute x3, waiting for transfers between devices: 7.54 us -> 5.09 us  [body(): lax.ppermute(image, 'row', [(i, (i + s) % rows) for i in range(rows)])]
    all_to_all x1, blocking collectives: 9.51 us -> 11.8 us  [body(): sums = lax.all_to_all(message, ('row', 'col'), 0, 0, tiled=True)]
    unnamed x20 -> x14, local copies, waits for them, and re-layouts: 3.5 us -> 2.95 us
where the time goes in v2:
time: 92.9 us; the launch traced here: 92.6 us
  Pallas kernels  51.9 us (56%)
  starting transfers between devices  14.5 us (16%)
  blocking collectives  11.8 us (13%)
  waiting for transfers between devices  10.7 us (12%)
  local copies, waits for them, and re-layouts  2.96 us (3%)
    pallas_call x2, Pallas kernels, rows_product(): call(functools.partial(rows_kernel, geo, lo, hi, have, stay, split), name...  24.3 us
    pallas_call x1, Pallas kernels, body(): call(functools.partial(cols_kernel, geo, have, len(parts)), 'cols_product...  23.7 us
    all_to_all x1, blocking collectives, body(): sums = lax.all_to_all(message, ('row', 'col'), 0, 0, tiled=True)  11.8 us
    ppermute x3, starting transfers between devices, body(): lax.ppermute(image, 'row', [(i, (i + s) % rows) for i in range(rows)])  6.01 us
    ppermute x3, waiting for transfers between devices, body(): lax.ppermute(image, 'row', [(i, (i + s) % rows) for i in range(rows)])  5.09 us
    ppermute x3, starting transfers between devices, body(): lax.ppermute(pair, 'col', flips(s))  4.35 us
    ppermute x3, starting transfers between devices, body(): lax.ppermute(sums[t], 'col', flips(2 * t))  3.55 us
    ppermute x3, waiting for transfers between devices, body(): lax.ppermute(sums[t], 'col', flips(2 * t))  3.32 us
  transfers between devices with their start and end apart: 11, of which 7 were waited for; matrix products, arithmetic and copies ran while one was open for 0% of the time, Pallas kernels for 10%

profile of v2, /device:TPU:0, one launch (start us, length us, event | category | flops | bytes accessed | tf_op | source)
XLA Modules:
  0.0 92.6 jit_solution(9347180905718181759)
XLA Ops:
  0.6 0.7 copy-done
  1.3 0.7 copy-done.2
  2.5 0.8 collective-permute-done.b
  3.4 2.8 %collective-permute-start.1 = (f32[8,768]{1,0:T(8,128)S(1)}, f32[8,768]{1,0:T(8,128)S(1)}, u32[]{:S(2)}, u32[]{:S(2)}) collective-permute-start(f32[8,768]{1,0:T(8,128)S(1)} %merge.1.refs_1_), channel_id=1, source_target_pairs={{0,2},{1,3},{2,0},{3,1},{4,6},{5,7},{6,4},{7,5},{8,10},{9,11},{10,... | collective-permute-start | bytes 73736 | tf_op jit(solution)/shard_map/ppermute | solution.py:460
  6.2 1.5 %collective-permute-start.2 = (f32[8,768]{1,0:T(8,128)S(1)}, f32[8,768]{1,0:T(8,128)S(1)}, u32[]{:S(2)}, u32[]{:S(2)}) collective-permute-start(f32[8,768]{1,0:T(8,128)S(1)} %merge.1.refs_1_), channel_id=1, source_target_pairs={{0,4},{1,5},{2,6},{3,7},{4,0},{5,1},{6,2},{7,3},{8,12},{9,13},{10,... | collective-permute-start | bytes 73736 | tf_op jit(solution)/shard_map/ppermute | solution.py:460
  7.7 2.9 %prefetch.1.refs_2_ = f32[3584,3072]{1,0:T(8,128)S(1)} custom-call(f32[6144,3072]{1,0:T(8,128)} %refs_0_.5, f32[4,768]{1,0:T(4,128)S(1)} %pack.1.a.after), custom_call_target="tpu_custom_call" | custom-call | tf_op jit(solution)/shard_map/prefetch/pallas_call | solution.py:448
  10.6 6.7 %rows_begin.1 = (f32[3,8,3072]{2,1,0:T(8,128)S(1)}, f32[3584,3072]{1,0:T(8,128)S(1)}) custom-call(f32[6144,3072]{1,0:T(8,128)} %refs_0_.5, f32[8,768]{1,0:T(8,128)S(1)} %merge.1.refs_1_, f32[3584,3072]{1,0:T(8,128)S(1)} %prefetch.1.refs_2_), custom_call_target="tpu_custom_call", output_to_operand_aliasing={{1}: (2, {})} | custom-call | tf_op jit(solution)/shard_map/rows_begin/pallas_call | solution.py:432
  17.4 17.6 %rows_rest.1 = (f32[8,3072]{1,0:T(8,128)}, f32[3584,3072]{1,0:T(8,128)S(1)}) custom-call(f32[6144,3072]{1,0:T(8,128)} %refs_0_.5, f32[8,768]{1,0:T(8,128)S(1)} %merge.1.refs_1_, f32[8,768]{1,0:T(8,128)S(1)} %collective-permute-done.1.refs_2_, f32[8,768]{1,0:T(8,128)S(1)} %collective-permute-done.2.refs_3_, ...), custom_call_target="tpu_custom_call", output_to_operand_aliasing={{1}: (6, {})} | custom-call | tf_op jit(solution)/shard_map/rows_rest/pallas_call | solution.py:432
  34.9 2.1 %collective-permute-start.4 = (f32[8,3072]{1,0:T(8,128)}, f32[8,3072]{1,0:T(8,128)S(1)}, u32[]{:S(2)}, u32[]{:S(2)}) collective-permute-start(f32[8,3072]{1,0:T(8,128)} %get-tuple-element.17.refs_2_), channel_id=1, source_target_pairs={{0,8},{8,16},{16,24},{24,0},{1,9},{9,17},{17,25},{25,1},{2,10},{10... | collective-permute-start | bytes 294920 | tf_op jit(solution)/shard_map/ppermute | solution.py:481
  37.0 2.6 %collective-permute-start.5 = (f32[8,3072]{1,0:T(8,128)}, f32[8,3072]{1,0:T(8,128)S(1)}, u32[]{:S(2)}, u32[]{:S(2)}) collective-permute-start(f32[8,3072]{1,0:T(8,128)} %get-tuple-element.17.refs_2_), channel_id=1, source_target_pairs={{0,16},{8,24},{16,0},{24,8},{1,17},{9,25},{17,1},{25,9},{2,18},{10... | collective-permute-start | bytes 294920 | tf_op jit(solution)/shard_map/ppermute | solution.py:481
  39.6 1.3 %collective-permute-start.6 = (f32[8,3072]{1,0:T(8,128)}, f32[8,3072]{1,0:T(8,128)S(1)}, u32[]{:S(2)}, u32[]{:S(2)}) collective-permute-start(f32[8,3072]{1,0:T(8,128)} %get-tuple-element.17.refs_2_), channel_id=1, source_target_pairs={{0,24},{8,0},{16,8},{24,16},{1,25},{9,1},{17,9},{25,17},{2,26},{10... | collective-permute-start | bytes 294920 | tf_op jit(solution)/shard_map/ppermute | solution.py:481
  41.0 2.0 %collective-permute-done.4.refs_3_ = f32[8,3072]{1,0:T(8,128)S(1)} collective-permute-done((f32[8,3072]{1,0:T(8,128)}, f32[8,3072]{1,0:T(8,128)S(1)}, u32[]{:S(2)}, u32[]{:S(2)}) %collective-permute-start.4) | collective-permute-done | bytes 98336 | tf_op jit(solution)/shard_map/ppermute | solution.py:481
  43.0 3.0 %collective-permute-done.5.refs_4_ = f32[8,3072]{1,0:T(8,128)S(1)} collective-permute-done((f32[8,3072]{1,0:T(8,128)}, f32[8,3072]{1,0:T(8,128)S(1)}, u32[]{:S(2)}, u32[]{:S(2)}) %collective-permute-start.5) | collective-permute-done | bytes 98336 | tf_op jit(solution)/shard_map/ppermute | solution.py:481
  46.1 0.6 copy-done.5
  46.7 23.7 %cols_product.1 = (f32[4,8,768]{2,1,0:T(8,128)}, f32[4,8,768]{2,1,0:T(8,128)}) custom-call(f32[6144,3072]{1,0:T(8,128)} %refs_0_.5, f32[3584,3072]{1,0:T(8,128)S(1)} %get-tuple-element.16.refs_1_, f32[8,3072]{1,0:T(8,128)} %get-tuple-element.17.refs_2_, f32[8,3072]{1,0:T(8,128)} %copy-done.4, f32[8,3072]{1,0:T(8,128)} %copy-done.5, f32[8,3072]{1,0:T(8,128)} %copy-done.6), custom_call_target="tpu_custom_call" | custom-call | tf_op jit(solution)/shard_map/cols_product/pallas_call | solution.py:484
  70.5 1.5 %collective-permute-done.7.b = f32[4,8,768]{2,1,0:T(8,128)S(1)} collective-permute-done((f32[4,8,768]{2,1,0:T(8,128)}, f32[4,8,768]{2,1,0:T(8,128)S(1)}, u32[]{:S(2)}, u32[]{:S(2)}) %collective-permute-start.7) | collective-permute-done | bytes 98336 | tf_op jit(solution)/shard_map/ppermute | solution.py:501
  72.0 0.9 copy-done.1
  72.9 2.5 %collective-permute-start.10 = (f32[8,768]{1,0:T(8,128)S(1)}, f32[8,768]{1,0:T(8,128)S(1)}, u32[]{:S(2)}, u32[]{:S(2)}) collective-permute-start(f32[8,768]{1,0:T(8,128)S(1)} %get-tuple-element.23), channel_id=1, source_target_pairs={{0,6},{1,7},{2,4},{3,5},{4,2},{5,3},{6,0},{7,1},{8,14},{9,15},{10,... | collective-permute-start | bytes 73736 | tf_op jit(solution)/shard_map/ppermute | solution.py:510
  75.5 0.5 collective-permute-start.8
  76.5 1.2 %collective-permute-done.10.refs_3_ = f32[8,768]{1,0:T(8,128)S(1)} collective-permute-done((f32[8,768]{1,0:T(8,128)S(1)}, f32[8,768]{1,0:T(8,128)S(1)}, u32[]{:S(2)}, u32[]{:S(2)}) %collective-permute-start.10) | collective-permute-done | bytes 24608 | tf_op jit(solution)/shard_map/ppermute | solution.py:510
  77.7 1.6 %collective-permute-done.8.refs_1_ = f32[8,768]{1,0:T(8,128)S(1)} collective-permute-done((f32[8,768]{1,0:T(8,128)S(1)}, f32[8,768]{1,0:T(8,128)S(1)}, u32[]{:S(2)}, u32[]{:S(2)}) %collective-permute-start.8) | collective-permute-done | bytes 24608 | tf_op jit(solution)/shard_map/ppermute | solution.py:510
  79.3 0.5 collective-permute-done.9.refs_2_
  80.1 11.8 %all_to_all.5.sums = f32[32,1,128]{2,1,0:T(1,128)S(1)} all-to-all(f32[32,1,128]{2,1,0:T(1,128)S(1)} %get-tuple-element.25), channel_id=1, replica_groups=mesh['row'=4,'col'=8] {'row','col'}, dimensions={0} | all-to-all | bytes 32768 | tf_op jit(solution)/shard_map/all_to_all | solution.py:525
  91.8 0.8 second_step.1
  (23 shorter events, 1.4 us)
Async XLA Ops:
  0.6 0.7 copy-start
  1.3 0.7 copy-start.2
  2.0 1.3 %collective-permute-start = (f32[4,768]{1,0:T(4,128)S(1)}, f32[4,768]{1,0:T(4,128)S(1)}, u32[]{:S(2)}, u32[]{:S(2)}) collective-permute-start(f32[4,768]{1,0:T(4,128)S(1)} %pack.1.a.after), channel_id=1, source_target_pairs={{0,1},{1,0},{2,3},{3,2},{4,5},{5,4},{6,7},{7,6},{8,9},{9,8},{10,11... | collective-permute-start | bytes 36872 | tf_op jit(solution)/shard_map/ppermute | solution.py:447
  3.4 14.0 %collective-permute-start.1 = (f32[8,768]{1,0:T(8,128)S(1)}, f32[8,768]{1,0:T(8,128)S(1)}, u32[]{:S(2)}, u32[]{:S(2)}) collective-permute-start(f32[8,768]{1,0:T(8,128)S(1)} %merge.1.refs_1_), channel_id=1, source_target_pairs={{0,2},{1,3},{2,0},{3,1},{4,6},{5,7},{6,4},{7,5},{8,10},{9,11},{10,... | collective-permute-start | bytes 73736 | tf_op jit(solution)/shard_map/ppermute | solution.py:460
  6.2 11.2 %collective-permute-start.2 = (f32[8,768]{1,0:T(8,128)S(1)}, f32[8,768]{1,0:T(8,128)S(1)}, u32[]{:S(2)}, u32[]{:S(2)}) collective-permute-start(f32[8,768]{1,0:T(8,128)S(1)} %merge.1.refs_1_), channel_id=1, source_target_pairs={{0,4},{1,5},{2,6},{3,7},{4,0},{5,1},{6,2},{7,3},{8,12},{9,13},{10,... | collective-permute-start | bytes 73736 | tf_op jit(solution)/shard_map/ppermute | solution.py:460
  7.7 9.7 %collective-permute-start.3 = (f32[8,768]{1,0:T(8,128)S(1)}, f32[8,768]{1,0:T(8,128)S(1)}, u32[]{:S(2)}, u32[]{:S(2)}) collective-permute-start(f32[8,768]{1,0:T(8,128)S(1)} %merge.1.refs_1_), channel_id=1, source_target_pairs={{0,6},{1,7},{2,4},{3,5},{4,2},{5,3},{6,0},{7,1},{8,14},{9,15},{10,... | collective-permute-start | bytes 73736 | tf_op jit(solution)/shard_map/ppermute | solution.py:460
  34.9 8.1 %collective-permute-start.4 = (f32[8,3072]{1,0:T(8,128)}, f32[8,3072]{1,0:T(8,128)S(1)}, u32[]{:S(2)}, u32[]{:S(2)}) collective-permute-start(f32[8,3072]{1,0:T(8,128)} %get-tuple-element.17.refs_2_), channel_id=1, source_target_pairs={{0,8},{8,16},{16,24},{24,0},{1,9},{9,17},{17,25},{25,1},{2,10},{10... | collective-permute-start | bytes 294920 | tf_op jit(solution)/shard_map/ppermute | solution.py:481
  37.0 9.0 %collective-permute-start.5 = (f32[8,3072]{1,0:T(8,128)}, f32[8,3072]{1,0:T(8,128)S(1)}, u32[]{:S(2)}, u32[]{:S(2)}) collective-permute-start(f32[8,3072]{1,0:T(8,128)} %get-tuple-element.17.refs_2_), channel_id=1, source_target_pairs={{0,16},{8,24},{16,0},{24,8},{1,17},{9,25},{17,1},{25,9},{2,18},{10... | collective-permute-start | bytes 294920 | tf_op jit(solution)/shard_map/ppermute | solution.py:481
  39.6 6.4 %collective-permute-start.6 = (f32[8,3072]{1,0:T(8,128)}, f32[8,3072]{1,0:T(8,128)S(1)}, u32[]{:S(2)}, u32[]{:S(2)}) collective-permute-start(f32[8,3072]{1,0:T(8,128)} %get-tuple-element.17.refs_2_), channel_id=1, source_target_pairs={{0,24},{8,0},{16,8},{24,16},{1,25},{9,1},{17,9},{25,17},{2,26},{10... | collective-permute-start | bytes 294920 | tf_op jit(solution)/shard_map/ppermute | solution.py:481
  43.0 3.0 %copy-start.4 = (f32[8,3072]{1,0:T(8,128)}, f32[8,3072]{1,0:T(8,128)S(1)}, u32[]{:S(2)}) copy-start(f32[8,3072]{1,0:T(8,128)S(1)} %collective-permute-done.4.refs_3_) | copy-start | bytes 294916
  46.1 0.6 copy-start.5
  46.1 0.7 copy-start.6
  46.7 29.8 %copy-start.3 = (f32[768]{0:T(1024)S(1)}, f32[768]{0:T(1024)}, u32[]{:S(2)}) copy-start(f32[768]{0:T(1024)} %width.1) | copy-start | bytes 9220
  70.5 1.6 %collective-permute-start.7 = (f32[4,8,768]{2,1,0:T(8,128)}, f32[4,8,768]{2,1,0:T(8,128)S(1)}, u32[]{:S(2)}, u32[]{:S(2)}) collective-permute-start(f32[4,8,768]{2,1,0:T(8,128)} %get-tuple-element.19), channel_id=1, source_target_pairs={{0,1},{1,0},{2,3},{3,2},{4,5},{5,4},{6,7},{7,6},{8,9},{9,8},{10,11... | collective-permute-start | bytes 294920 | tf_op jit(solution)/shard_map/ppermute | solution.py:501
  72.0 0.9 copy-start.1
  72.9 4.8 %collective-permute-start.10 = (f32[8,768]{1,0:T(8,128)S(1)}, f32[8,768]{1,0:T(8,128)S(1)}, u32[]{:S(2)}, u32[]{:S(2)}) collective-permute-start(f32[8,768]{1,0:T(8,128)S(1)} %get-tuple-element.23), channel_id=1, source_target_pairs={{0,6},{1,7},{2,4},{3,5},{4,2},{5,3},{6,0},{7,1},{8,14},{9,15},{10,... | collective-permute-start | bytes 73736 | tf_op jit(solution)/shard_map/ppermute | solution.py:510
  75.5 3.8 %collective-permute-start.8 = (f32[8,768]{1,0:T(8,128)S(1)}, f32[8,768]{1,0:T(8,128)S(1)}, u32[]{:S(2)}, u32[]{:S(2)}) collective-permute-start(f32[8,768]{1,0:T(8,128)S(1)} %get-tuple-element.21), channel_id=1, source_target_pairs={{0,2},{1,3},{2,0},{3,1},{4,6},{5,7},{6,4},{7,5},{8,10},{9,11},{10,... | collective-permute-start | bytes 73736 | tf_op jit(solution)/shard_map/ppermute | solution.py:510
  76.0 3.8 %collective-permute-start.9 = (f32[8,768]{1,0:T(8,128)S(1)}, f32[8,768]{1,0:T(8,128)S(1)}, u32[]{:S(2)}, u32[]{:S(2)}) collective-permute-start(f32[8,768]{1,0:T(8,128)S(1)} %get-tuple-element.22), channel_id=1, source_target_pairs={{0,4},{1,5},{2,6},{3,7},{4,0},{5,1},{6,2},{7,3},{8,12},{9,13},{10,... | collective-permute-start | bytes 73736 | tf_op jit(solution)/shard_map/ppermute | solution.py:510
